TPU v7x, 32 devices: a whole 2x2x4 slice. The times are simulated.
32 devices in a mesh: grp: 2 (over x), tm: 16 (over z, y, core).
Axes of the slice: x: 2, y: 2, z: 4, core: 2. Of those that a mesh axis runs over, the one named last changes fastest.
Arguments:
- samples: bfloat16 [16, 2097152], P('grp', 'tm'), parts along dimension 0, may hold values from -128 to 127, as said below
- filter_taps: bfloat16 [16, 8192], replicated, may hold values from -4 to 4
Outputs:
- channelized: bfloat16 [16, 2, 4096, 256], P('grp', None, 'tm'), parts along dimension 0
There are 2 independent parts, one for each index of `grp`. A program takes and returns all parts, laid end to end along the dimension named above; an argument that names none is the same for every part. Nothing has to cross between parts.
Inputs may be any that keep to these rules, and one draw needn't show every extreme that they name: `samples`: every sample is a whole number, as from an 8-bit converter.
All inputs are finite; a program needn't handle non-finite values.
Results may differ from a plain program's by a relative error of at most 0.007.
Values may be sent and summed in bfloat16 or wider, within the bound.
A program may use at most 128 MiB of HBM per device.

v0:
```python
import jax
import jax.numpy as jnp
from jax import lax
from jax.sharding import PartitionSpec as P

ROW_LEN = 128
target_level = 0.378
epsilon = 1e-06


def shifted(value, axis, by):
    size = lax.axis_size(axis)
    pairs = [(i, i + by) for i in range(size) if 0 <= i + by < size]
    return lax.ppermute(value, axis, pairs)


def tables(row_len, col_len):
    fft_len = row_len * col_len
    rows_a = jnp.arange(row_len, dtype=jnp.int32)
    cols_b = jnp.arange(col_len, dtype=jnp.int32)
    half_c = jnp.arange(col_len // 2, dtype=jnp.int32)
    angle_a = (
        2.0 * jnp.pi / row_len * (rows_a[:, None] * rows_a[None, :] % row_len).astype(jnp.float32)
    )
    angle_t = (
        2.0 * jnp.pi / fft_len * (cols_b[:, None] * rows_a[None, :] % fft_len).astype(jnp.float32)
    )
    angle_b = (
        2.0 * jnp.pi / col_len * (cols_b[:, None] * half_c[None, :] % col_len).astype(jnp.float32)
    )
    return (
        jnp.cos(angle_a).astype(jnp.bfloat16),
        jnp.sin(angle_a).astype(jnp.bfloat16),
        jnp.cos(angle_t),
        jnp.sin(angle_t),
        jnp.cos(angle_b).astype(jnp.bfloat16),
        jnp.sin(angle_b).astype(jnp.bfloat16),
    )


def transform(filtered):
    streams, frames, fft_len = filtered.shape
    col_len = fft_len // ROW_LEN
    cos_a, sin_a, cos_t, sin_t, cos_b, sin_b = tables(ROW_LEN, col_len)
    blocks = filtered.reshape(streams, frames, ROW_LEN, col_len)
    first_re = jnp.einsum("sfab,ad->sfbd", blocks, cos_a, preferred_element_type=jnp.float32)
    first_im = -jnp.einsum("sfab,ad->sfbd", blocks, sin_a, preferred_element_type=jnp.float32)
    twisted_re = (first_re * cos_t + first_im * sin_t).astype(jnp.bfloat16)
    twisted_im = (first_im * cos_t - first_re * sin_t).astype(jnp.bfloat16)
    spec_re = jnp.einsum(
        "sfbd,bc->scdf", twisted_re, cos_b, preferred_element_type=jnp.float32
    ) + jnp.einsum("sfbd,bc->scdf", twisted_im, sin_b, preferred_element_type=jnp.float32)
    spec_im = jnp.einsum(
        "sfbd,bc->scdf", twisted_im, cos_b, preferred_element_type=jnp.float32
    ) - jnp.einsum("sfbd,bc->scdf", twisted_re, sin_b, preferred_element_type=jnp.float32)
    return (spec_re.reshape(streams, -1, frames), spec_im.reshape(streams, -1, frames))


def on_device(samples, filter_taps):
    streams = samples.shape[0]
    tap_count, fft_len = filter_taps.shape
    frames = samples.shape[1] // fft_len
    signal = samples.reshape(streams, frames, fft_len)
    history = shifted(signal[:, frames - (tap_count - 1) :, :], "tm", 1)
    extended = jnp.concatenate([history, signal], axis=1)
    weights = filter_taps.astype(jnp.float32)
    filtered = jnp.zeros((streams, frames, fft_len), jnp.float32)
    for tap_index in range(tap_count):
        offset = tap_count - 1 - tap_index
        filtered = filtered + weights[tap_index] * extended[:, offset : offset + frames].astype(
            jnp.float32
        )
    filtered = filtered.astype(jnp.bfloat16)
    spec_re, spec_im = transform(filtered)
    real_part = spec_re.astype(jnp.bfloat16)
    imag_part = spec_im.astype(jnp.bfloat16)
    real_wide = real_part.astype(jnp.float32)
    imag_wide = imag_part.astype(jnp.float32)
    local_power = jnp.sum(real_wide * real_wide + imag_wide * imag_wide, axis=(1, 2))
    total_power = lax.psum(local_power, "tm")
    count = frames * lax.axis_size("tm") * spec_re.shape[1]
    gain = target_level / jnp.sqrt(total_power / count + epsilon)
    scaled = jnp.stack(
        [
            jnp.clip(real_wide * gain[:, None, None], -1.0, 1.0),
            jnp.clip(imag_wide * gain[:, None, None], -1.0, 1.0),
        ],
        axis=1,
    ).astype(jnp.bfloat16)
    result = lax.all_to_all(scaled, "tm", split_axis=2, concat_axis=3, tiled=True)
    return result


def solution(mesh):
    return jax.shard_map(
        on_device,
        mesh=mesh,
        in_specs=(P("grp", "tm"), P()),
        out_specs=P("grp", None, "tm", None),
        check_vma=False,
    )
```

profile of v0, /device:TPU:1, one launch (start us, length us, event | category | flops | bytes accessed | tf_op | source)
XLA Modules:
  0.0 244.5 jit_solution(3988610349749079119)
XLA Ops:
  0.0 1.8 slice.130
  1.8 4.5 %collective-permute-start = (bf16[8,15,8192]{2,0,1:T(8,128)(2,1)S(1)}, bf16[8,15,8192]{2,0,1:T(8,128)(2,1)S(1)}, u32[]{:S(2)}, u32[]{:S(2)}) collective-permute-start(bf16[8,15,8192]{2,0,1:T(8,128)(2,1)S(1)} %slice.130), channel_id=1, source_target_pairs={{0,1},{1,2},{2,3},{3,4},{4,5},{5,6},{6,7},{7,8},{8,9},{9,10},{10,1... | collective-permute-start | bytes 5898248 | tf_op jit(solution)/shard_map/ppermute | solution.py:14
  7.0 20.9 %collective-permute-done = bf16[8,15,8192]{2,0,1:T(8,128)(2,1)S(1)} collective-permute-done((bf16[8,15,8192]{2,0,1:T(8,128)(2,1)S(1)}, bf16[8,15,8192]{2,0,1:T(8,128)(2,1)S(1)}, u32[]{:S(2)}, u32[]{:S(2)}) %collective-permute-start) | collective-permute-done | bytes 1966112 | tf_op jit(solution)/shard_map/ppermute | solution.py:14
  27.9 8.7 %add_convert_fusion.1 = bf16[8,16,8192]{2,0,1:T(8,128)(2,1)S(1)} fusion(bf16[8,16,8192]{2,0,1:T(8,128)(2,1)S(1)} %bitcast.84, bf16[8,15,8192]{2,0,1:T(8,128)(2,1)S(1)} %collective-permute-done, f32[8192]{0:T(1024)S(1)} %bitcast.100, f32[8192]{0:T(1024)S(1)} %bitcast.99, f32[8192]{0:T(1024)S(1)} %bitcast.98, f32[8192]{0:T(1024)S(1)} %bitcast.97, ...), kind=kLoop, calls=%fused_computation.30 | loop fusion | flops 66060288 | bytes 6684672 | tf_op jit(solution)/shard_map/convert_element_type | solution.py:73
  36.6 1.2 copy.27
  37.8 5.5 %reshape.106 = bf16[8,16,128,64]{3,2,1,0:T(8,128)(2,1)} reshape(bf16[8,16,8192]{2,1,0:T(8,128)(2,1)S(1)} %copy.27) | data formatting | bytes 4194304 | tf_op jit(solution)/shard_map/reshape | solution.py:45
  43.3 3.7 %fusion.33 = f32[8,16,64,128]{3,2,1,0:T(8,128)S(1)} fusion(bf16[8,16,128,64]{3,2,1,0:T(8,128)(2,1)} %reshape.106), kind=kOutput, calls=%fused_computation.81 | convolution fusion | flops 268681216 | bytes 6291456 | tf_op jit(solution)/shard_map/sfab,ad->sfbd/dot_general | solution.py:47
  47.0 1.7 add_convert_fusion
  48.8 0.5 fusion.54
  49.3 0.5 fusion.52
  49.8 0.5 add_convert_fusion.2
  50.3 1.6 convert_bitcast_fusion
  51.9 0.8 fusion.1
  52.7 30.6 %psum.7 = f32[8]{0:T(128)S(1)} all-reduce(f32[8]{0:T(128)S(1)} %get-tuple-element.25), channel_id=1, replica_groups=mesh['grp'=2,'tm'=16] {'tm'}, use_global_device_ids=true, to_apply=%region_1.2 | all-reduce | flops 8 | bytes 64 | tf_op jit(solution)/shard_map/psum | solution.py:80
  83.4 1.8 reshape.107
  85.1 1.6 convert_bitcast_fusion.1
  86.7 2.7 %reshape.108 = f32[8,1,4096,16]{2,3,0,1:T(8,128)} reshape(f32[8,32,128,16]{2,1,3,0:T(8,128)} %convert_bitcast_fusion.1) | data formatting | bytes 4194304 | tf_op jit(solution)/shard_map/convert_element_type | solution.py:78
  89.5 2.0 fusion.19
  91.7 27.8 %copy.32 = bf16[8,2,4096,16]{3,1,0,2:T(2,128)(2,1)} copy(bf16[8,2,4096,16]{2,3,1,0:T(8,128)(2,1)S(1)} %pad_maximum_fusion.1) | data formatting | bytes 4194304 | tf_op jit(solution)/shard_map/stack | solution.py:83
  119.5 19.7 %reshape.113 = bf16[16,2,32768]{2,1,0:T(2,128)(2,1)S(1)} reshape(bf16[4096,8,2,16]{3,2,1,0:T(2,128)(2,1)} %bitcast.80) | data formatting | bytes 4194304
  139.3 51.1 %all_to_all.18 = bf16[16,2,32768]{2,1,0:T(2,128)(2,1)} all-to-all(bf16[16,2,32768]{2,1,0:T(2,128)(2,1)S(1)} %reshape.113), channel_id=1, replica_groups=mesh['grp'=2,'tm'=16] {'tm'}, dimensions={0} | all-to-all | bytes 4194304 | tf_op jit(solution)/shard_map/all_to_all | solution.py:90
  190.4 16.5 %reshape.114 = bf16[4096,8,2,16]{3,2,1,0:T(2,128)(2,1)} reshape(bf16[16,2,32768]{2,1,0:T(2,128)(2,1)} %all_to_all.18) | data formatting | bytes 4194304
  206.8 35.3 %copy.43 = bf16[8,2,16,256,16]{3,4,2,1,0:T(8,128)(2,1)S(1)} copy(bf16[8,2,16,256,16]{4,1,0,3,2:T(2,128)(2,1)} %bitcast.81) | data formatting | bytes 4194304 | tf_op jit(solution)/shard_map/all_to_all | solution.py:90
  242.1 2.4 copy.35
  (10 shorter events, 0.8 us)
Async XLA Ops:
  0.0 6.5 %copy-start.2 = (bf16[16,8192]{1,0:T(8,128)(2,1)S(1)}, bf16[16,8192]{1,0:T(8,128)(2,1)}, u32[]{:S(2)}) copy-start(bf16[16,8192]{1,0:T(8,128)(2,1)} %param.3) | copy-start | bytes 786436
  0.0 27.9 %copy-start.1 = (bf16[8,131072]{1,0:T(8,128)(2,1)S(1)}, bf16[8,131072]{1,0:T(8,128)(2,1)}, u32[]{:S(2)}) copy-start(bf16[8,131072]{1,0:T(8,128)(2,1)} %param.2) | copy-start | bytes 6291460
  1.8 26.1 %collective-permute-start = (bf16[8,15,8192]{2,0,1:T(8,128)(2,1)S(1)}, bf16[8,15,8192]{2,0,1:T(8,128)(2,1)S(1)}, u32[]{:S(2)}, u32[]{:S(2)}) collective-permute-start(bf16[8,15,8192]{2,0,1:T(8,128)(2,1)S(1)} %slice.130), channel_id=1, source_target_pairs={{0,1},{1,2},{2,3},{3,4},{4,5},{5,6},{6,7},{7,8},{8,9},{9,10},{10,1... | collective-permute-start | bytes 5898248 | tf_op jit(solution)/shard_map/ppermute | solution.py:14
  43.3 3.7 %copy-start = (bf16[8,16,128,64]{3,2,1,0:T(8,128)(2,1)S(1)}, bf16[8,16,128,64]{3,2,1,0:T(8,128)(2,1)}, u32[]{:S(2)}) copy-start(bf16[8,16,128,64]{3,2,1,0:T(8,128)(2,1)} %reshape.106) | copy-start | bytes 6291460
where the time goes:
time: 246 us; the launch traced here: 244 us
  local copies, waits for them, and re-layouts  115 us (47%)
  blocking collectives  81.7 us (33%)
  waiting for transfers between devices  20.9 us (8%)
  other arithmetic  14.3 us (6%)
  matrix products  7.76 us (3%)
  starting transfers between devices  4.53 us (2%)
    all_to_all x1, blocking collectives, on_device(): lax.all_to_all(scaled, 'tm', split_axis=2, concat_axis=3, tiled=True)  51.1 us
    all_to_all x2, local copies, waits for them, and re-layouts, on_device(): lax.all_to_all(scaled, 'tm', split_axis=2, concat_axis=3, tiled=True)  37.7 us
    unnamed x8, local copies, waits for them, and re-layouts  36.2 us
    psum x1, blocking collectives, on_device(): total_power = lax.psum(local_power, 'tm')  30.6 us
    another operation x1, local copies, waits for them, and re-layouts, on_device(): jnp.stack([jnp.clip(real_wide * gain[:, None, None], -1.0, 1.0), jnp.clip...  27.8 us
    ppermute x1, waiting for transfers between devices, shifted(): return lax.ppermute(value, axis, pairs)  20.9 us
    convert_element_type x1, other arithmetic, on_device(): filtered = filtered.astype(jnp.bfloat16)  8.7 us
    reshape x1, local copies, waits for them, and re-layouts, transform(): blocks = filtered.reshape(streams, frames, ROW_LEN, col_len)  5.54 us
  transfers between devices with their start and end apart: 1, of which 1 were waited for; matrix products, arithmetic and copies ran while one was open for 0% of the time, Pallas kernels for 0%

commit v1 on v0

--- a/solution.py
+++ b/solution.py
@@ -77,7 +77,7 @@
     real_wide = real_part.astype(jnp.float32)
     imag_wide = imag_part.astype(jnp.float32)
     local_power = jnp.sum(real_wide * real_wide + imag_wide * imag_wide, axis=(1, 2))
-    total_power = lax.psum(local_power, "tm")
+    total_power = jnp.sum(lax.all_gather(local_power, "tm"), axis=0)
     count = frames * lax.axis_size("tm") * spec_re.shape[1]
     gain = target_level / jnp.sqrt(total_power / count + epsilon)
     scaled = jnp.stack(

time: 246 us -> 255 us (1.037)
  other arithmetic: 14.3 us -> 20.9 us
    psum x1 -> x0, blocking collectives: 30.6 us -> none  [on_device(): total_power = lax.psum(local_power, 'tm')]
    unnamed x0 -> x1, blocking collectives: none -> 30.6 us
    convert_element_type x1, other arithmetic: 8.7 us -> 15.3 us  [on_device(): filtered = filtered.astype(jnp.bfloat16)]
    unnamed x8 -> x13, local copies, waits for them, and re-layouts: 36.2 us -> 37.1 us
  transfers between devices with their start and end apart: 1 -> 1, of which waited for: 1 -> 1; matrix products, arithmetic and copies ran while one was open for 0% -> 1% of each run, Pallas kernels for 0% -> 0%
where the time goes in v1:
time: 255 us; the launch traced here: 253 us
  local copies, waits for them, and re-layouts  117 us (46%)
  blocking collectives  81.7 us (32%)
  other arithmetic  20.9 us (8%)
  waiting for transfers between devices  19.9 us (8%)
  matrix products  7.77 us (3%)
  starting transfers between devices  4.52 us (2%)
    all_to_all x1, blocking collectives, on_device(): lax.all_to_all(scaled, 'tm', split_axis=2, concat_axis=3, tiled=True)  51.1 us
    all_to_all x2, local copies, waits for them, and re-layouts, on_device(): lax.all_to_all(scaled, 'tm', split_axis=2, concat_axis=3, tiled=True)  37.7 us
    unnamed x13, local copies, waits for them, and re-layouts  37.1 us
    unnamed x1, blocking collectives  30.6 us
    another operation x1, local copies, waits for them, and re-layouts, on_device(): jnp.stack([jnp.clip(real_wide * gain[:, None, None], -1.0, 1.0), jnp.clip...  27.8 us
    ppermute x1, waiting for transfers between devices, shifted(): return lax.ppermute(value, axis, pairs)  19.9 us
    convert_element_type x1, other arithmetic, on_device(): filtered = filtered.astype(jnp.bfloat16)  15.3 us
    reshape x1, local copies, waits for them, and re-layouts, transform(): blocks = filtered.reshape(streams, frames, ROW_LEN, col_len)  5.53 us
  transfers between devices with their start and end apart: 1, of which 1 were waited for; matrix products, arithmetic and copies ran while one was open for 1% of the time, Pallas kernels for 0%

profile of v1, /device:TPU:1, one launch (start us, length us, event | category | flops | bytes accessed | tf_op | source)
XLA Modules:
  0.0 253.0 jit_solution(13952734660045768836)
XLA Ops:
  0.0 3.1 %slice.130 = bf16[8,15,8192]{2,0,1:T(8,128)(2,1)} slice(bf16[8,16,8192]{2,0,1:T(8,128)(2,1)} %bitcast.84), slice={[0:8], [1:16], [0:8192]} | slice | bytes 3932160 | tf_op jit(solution)/shard_map/slice | solution.py:64
  3.2 4.5 %collective-permute-start = (bf16[8,15,8192]{2,0,1:T(8,128)(2,1)}, bf16[8,15,8192]{2,0,1:T(8,128)(2,1)}, u32[]{:S(2)}, u32[]{:S(2)}) collective-permute-start(bf16[8,15,8192]{2,0,1:T(8,128)(2,1)} %slice.130), channel_id=1, source_target_pairs={{0,1},{1,2},{2,3},{3,4},{4,5},{5,6},{6,7},{7,8},{8,9},{9,10},{10,1... | collective-permute-start | bytes 5898248 | tf_op jit(solution)/shard_map/ppermute | solution.py:14
  7.7 0.7 dynamic-slice
  9.7 19.9 %collective-permute-done = bf16[8,15,8192]{2,0,1:T(8,128)(2,1)} collective-permute-done((bf16[8,15,8192]{2,0,1:T(8,128)(2,1)}, bf16[8,15,8192]{2,0,1:T(8,128)(2,1)}, u32[]{:S(2)}, u32[]{:S(2)}) %collective-permute-start) | collective-permute-done | bytes 1966112 | tf_op jit(solution)/shard_map/ppermute | solution.py:14
  29.6 15.3 %add_convert_fusion.1 = bf16[8,16,8192]{2,0,1:T(8,128)(2,1)S(1)} fusion(bf16[8,16,8192]{2,0,1:T(8,128)(2,1)S(1)} %bitcast.85, bf16[8,15,8192]{2,0,1:T(8,128)(2,1)} %collective-permute-done, f32[8192]{0:T(1024)S(1)} %bitcast.101, f32[8192]{0:T(1024)S(1)} %bitcast.100, f32[8192]{0:T(1024)S(1)} %bitcast.99, f32[8192]{0:T(1024)S(1)} %bitcast.98, ...), kind=kLoop, calls=%fused_computation.30 | loop fusion | flops 66060288 | bytes 6684672 | tf_op jit(solution)/shard_map/convert_element_type | solution.py:73
  44.8 1.2 copy.27
  46.0 5.5 %reshape.111 = bf16[8,16,128,64]{3,2,1,0:T(8,128)(2,1)} reshape(bf16[8,16,8192]{2,1,0:T(8,128)(2,1)S(1)} %copy.27) | data formatting | bytes 4194304 | tf_op jit(solution)/shard_map/reshape | solution.py:45
  51.5 3.7 %fusion.33 = f32[8,16,64,128]{3,2,1,0:T(8,128)S(1)} fusion(bf16[8,16,128,64]{3,2,1,0:T(8,128)(2,1)} %reshape.111), kind=kOutput, calls=%fused_computation.81 | convolution fusion | flops 268681216 | bytes 6291456 | tf_op jit(solution)/shard_map/sfab,ad->sfbd/dot_general | solution.py:47
  55.2 1.7 add_convert_fusion
  57.4 0.5 fusion.52
  58.0 0.5 add_convert_fusion.2
  58.5 1.6 convert_bitcast_fusion
  60.1 0.8 fusion.1
  61.1 30.6 %all-reduce = f32[128]{0:T(128)S(1)} all-reduce(f32[128]{0:T(128)S(1)} %dynamic-update-slice), channel_id=2, replica_groups=mesh['grp'=2,'tm'=16] {'tm'}, use_global_device_ids=true, to_apply=%add | all-reduce | flops 128 | bytes 1024
  91.8 1.8 reshape.112
  93.6 1.6 convert_bitcast_fusion.1
  95.2 2.8 %reshape.113 = f32[8,1,4096,16]{2,3,0,1:T(8,128)} reshape(f32[8,32,128,16]{2,1,3,0:T(8,128)} %convert_bitcast_fusion.1) | data formatting | bytes 4194304 | tf_op jit(solution)/shard_map/convert_element_type | solution.py:78
  98.0 2.0 fusion.19
  100.2 27.8 %copy.32 = bf16[8,2,4096,16]{3,1,0,2:T(2,128)(2,1)} copy(bf16[8,2,4096,16]{2,3,1,0:T(8,128)(2,1)S(1)} %pad_maximum_fusion.1) | data formatting | bytes 4194304 | tf_op jit(solution)/shard_map/stack | solution.py:83
  128.0 19.7 %reshape.124 = bf16[16,2,32768]{2,1,0:T(2,128)(2,1)S(1)} reshape(bf16[4096,8,2,16]{3,2,1,0:T(2,128)(2,1)} %bitcast.81) | data formatting | bytes 4194304
  147.8 51.1 %all_to_all.18 = bf16[16,2,32768]{2,1,0:T(2,128)(2,1)} all-to-all(bf16[16,2,32768]{2,1,0:T(2,128)(2,1)S(1)} %reshape.124), channel_id=1, replica_groups=mesh['grp'=2,'tm'=16] {'tm'}, dimensions={0} | all-to-all | bytes 4194304 | tf_op jit(solution)/shard_map/all_to_all | solution.py:90
  198.9 16.5 %reshape.125 = bf16[4096,8,2,16]{3,2,1,0:T(2,128)(2,1)} reshape(bf16[16,2,32768]{2,1,0:T(2,128)(2,1)} %all_to_all.18) | data formatting | bytes 4194304
  215.3 35.3 %copy.43 = bf16[8,2,16,256,16]{3,4,2,1,0:T(8,128)(2,1)S(1)} copy(bf16[8,2,16,256,16]{4,1,0,3,2:T(2,128)(2,1)} %bitcast.82) | data formatting | bytes 4194304 | tf_op jit(solution)/shard_map/all_to_all | solution.py:90
  250.6 2.4 copy.35
  (17 shorter events, 1.6 us)
Async XLA Ops:
  0.0 7.7 %copy-start.3 = (u32[32]{0:T(128)S(1)}, u32[32]{0:T(128)}, u32[]{:S(2)}) copy-start(u32[32]{0:T(128)} %constant.64) | copy-start | bytes 388
  0.0 9.2 %copy-start.2 = (bf16[16,8192]{1,0:T(8,128)(2,1)S(1)}, bf16[16,8192]{1,0:T(8,128)(2,1)}, u32[]{:S(2)}) copy-start(bf16[16,8192]{1,0:T(8,128)(2,1)} %param.3) | copy-start | bytes 786436
  0.0 29.5 %copy-start.1 = (bf16[8,131072]{1,0:T(8,128)(2,1)S(1)}, bf16[8,131072]{1,0:T(8,128)(2,1)}, u32[]{:S(2)}) copy-start(bf16[8,131072]{1,0:T(8,128)(2,1)} %param.2) | copy-start | bytes 6291460
  3.2 26.4 %collective-permute-start = (bf16[8,15,8192]{2,0,1:T(8,128)(2,1)}, bf16[8,15,8192]{2,0,1:T(8,128)(2,1)}, u32[]{:S(2)}, u32[]{:S(2)}) collective-permute-start(bf16[8,15,8192]{2,0,1:T(8,128)(2,1)} %slice.130), channel_id=1, source_target_pairs={{0,1},{1,2},{2,3},{3,4},{4,5},{5,6},{6,7},{7,8},{8,9},{9,10},{10,1... | collective-permute-start | bytes 5898248 | tf_op jit(solution)/shard_map/ppermute | solution.py:14
  51.5 3.7 %copy-start = (bf16[8,16,128,64]{3,2,1,0:T(8,128)(2,1)S(1)}, bf16[8,16,128,64]{3,2,1,0:T(8,128)(2,1)}, u32[]{:S(2)}) copy-start(bf16[8,16,128,64]{3,2,1,0:T(8,128)(2,1)} %reshape.111) | copy-start | bytes 6291460
